TPU v7x, 32 devices: a whole 2x2x4 slice. The times are simulated.
32 devices in a mesh: rep: 2 (over x), exp: 4 (over z), ten: 4 (over y, core).
Axes of the slice: x: 2, y: 2, z: 4, core: 2. Of those that a mesh axis runs over, the one named last changes fastest.
Arguments:
- hidden_in: bfloat16 [768, 3072], P(('rep', 'exp', 'ten')), parts along dimension 0, may hold values from -6 to 6
- queries: bfloat16 [768, 6144], P(('rep', 'exp', 'ten')), parts along dimension 0, may hold values from -100 to 100
- new_kv: bfloat16 [2, 768, 1024], P(None, ('rep', 'exp', 'ten')), parts along dimension 1, may hold values from -5 to 5
- prefix_kv: bfloat16 [2, 8, 128, 1024], P(None, ('rep', 'exp'), 'ten'), parts along dimension 1, may hold values from -5 to 5
- decode_kv: bfloat16 [2, 128, 48, 1024], P(None, ('rep', 'exp', 'ten')), parts along dimension 1, may hold values from -5 to 5
- prefix_len: int32 [8], P(('rep', 'exp')), parts along dimension 0, may hold values from 2 to 128
- decode_len: int32 [128], P(('rep', 'exp', 'ten')), parts along dimension 0, may hold values from 2 to 48
- out_proj: bfloat16 [6144, 3072], P('ten'), may hold values from -0.078125 to 0.078125
- norm_gain: float32 [3072], replicated, may hold values from 0.5 to 1.5
- router_w: bfloat16 [3072, 8], replicated, may hold values from -0.109375 to 0.109375
- expert_ids: int32 [768, 2], P(('rep', 'exp', 'ten')), parts along dimension 0, may hold values from 0 to 7, all different within a row; in each aligned block of 24 rows (0 to 23, 24 to 47, ...) at most 7 rows name the same one
- w_gate: bfloat16 [8, 3072, 8192], P('exp', None, 'ten'), may hold values from -0.109375 to 0.109375
- w_up: bfloat16 [8, 3072, 8192], P('exp', None, 'ten'), may hold values from -0.109375 to 0.109375
- w_down: bfloat16 [8, 8192, 3072], P('exp', 'ten'), may hold values from -0.0625 to 0.0625
Outputs:
- layer_out: bfloat16 [768, 3072], P(('rep', 'exp', 'ten')), parts along dimension 0
There are 2 independent parts, one for each index of `rep`. A program takes and returns all parts, laid end to end along the dimension named above; an argument that names none is the same for every part. Nothing has to cross between parts.
Inputs may be any that keep to these rules, and one draw needn't show every extreme that they name: `expert_ids`: each row names two different experts. Within each aligned block of 24 rows (the rows of one device) no expert is named by more than 7 rows, and in some block one expert is named by exactly 7 rows.
All inputs are finite; a program needn't handle non-finite values.
Results may differ from a plain program's by a relative error of at most 0.013.
Values may be sent and summed in bfloat16 or wider, within the bound.
No kernel may reach another device: no remote copies, remote signals or barrier semaphores. Data moves between devices by JAX's collectives and lax.ppermute only.
A program may use at most 128 MiB of HBM per device.

v0:
```python
import jax
import jax.numpy as jnp
from jax import lax
from jax.sharding import PartitionSpec as P

HD = 128
CAP = 7
lowest_score = -1e30


def local_softmax(scores, visible):
    masked = jnp.where(visible, scores, lowest_score)
    row_max = jnp.max(masked, axis=-1)
    exponent = jnp.where(visible, jnp.exp(masked - row_max[..., None]), 0.0)
    return (row_max, exponent, jnp.sum(exponent, axis=-1))


def on_device(
    hidden_in,
    queries,
    new_kv,
    prefix_kv,
    decode_kv,
    prefix_len,
    decode_len,
    out_proj,
    norm_gain,
    router_w,
    expert_ids,
    w_gate,
    w_up,
    w_down,
):
    ten_size = lax.axis_size("ten")
    groups = lax.axis_size("exp")
    my_ten = lax.axis_index("ten")
    rows_dev, model_width = hidden_in.shape
    dec_dev = decode_len.shape[0]
    span_dev = rows_dev - dec_dev
    span_rows = span_dev * ten_size
    kv_width = new_kv.shape[2]
    heads_kv = kv_width // HD
    heads_q = queries.shape[1] // HD
    per_kv = heads_q // heads_kv
    score_scale = HD ** (-0.5)
    ctx_len = decode_kv.shape[2]
    own_heads = queries.reshape(rows_dev, heads_kv, per_kv, HD)
    dec_keys = jnp.concatenate([decode_kv[0], new_kv[0, span_dev:, None]], axis=1).reshape(
        dec_dev, ctx_len + 1, heads_kv, HD
    )
    dec_values = jnp.concatenate([decode_kv[1], new_kv[1, span_dev:, None]], axis=1).reshape(
        dec_dev, ctx_len + 1, heads_kv, HD
    )
    dec_scores = (
        jnp.einsum(
            "dcgh,dpch->dcgp", own_heads[span_dev:], dec_keys, preferred_element_type=jnp.float32
        )
        * score_scale
    )
    dec_pos = jnp.arange(ctx_len + 1, dtype=jnp.int32)[None, :]
    dec_visible = ((dec_pos < decode_len[:, None]) | (dec_pos == ctx_len))[:, None, None, :]
    dec_max, dec_exponent, dec_totals = local_softmax(dec_scores, dec_visible)
    dec_partial = jnp.einsum(
        "dcgp,dpch->dcgh",
        dec_exponent.astype(jnp.bfloat16),
        dec_values,
        preferred_element_type=jnp.float32,
    )
    full_prefix, full_fresh = (
        lax.all_gather(prefix_kv[:, 0], "ten", axis=1, tiled=True),
        lax.all_gather(new_kv[:, :span_dev], "ten", axis=1, tiled=True),
    )
    prefix_total = full_prefix.shape[1]
    key_rows = jnp.concatenate([full_prefix[0], full_fresh[0]], axis=0).reshape(
        prefix_total + span_rows, heads_kv, HD
    )
    value_rows = jnp.concatenate([full_prefix[1], full_fresh[1]], axis=0).reshape(
        prefix_total + span_rows, heads_kv, HD
    )
    scores = (
        jnp.einsum(
            "rcgh,pch->rcgp", own_heads[:span_dev], key_rows, preferred_element_type=jnp.float32
        )
        * score_scale
    )
    query_row = my_ten * span_dev + jnp.arange(span_dev, dtype=jnp.int32)[:, None]
    positions = jnp.arange(prefix_total + span_rows, dtype=jnp.int32)[None, :]
    visible = jnp.where(
        positions < prefix_total, positions < prefix_len[0], positions - prefix_total <= query_row
    )[:, None, None, :]
    row_max, exponent, totals = local_softmax(scores, visible)
    span_out = (
        jnp.einsum(
            "rcgp,pch->rcgh",
            exponent.astype(jnp.bfloat16),
            value_rows,
            preferred_element_type=jnp.float32,
        )
        / totals[..., None]
    )
    dec_out = dec_partial / dec_totals[..., None]
    attended_rows = (
        jnp.concatenate([span_out, dec_out], axis=0)
        .reshape(rows_dev, heads_q * HD)
        .astype(jnp.bfloat16)
    )
    attended = lax.all_to_all(attended_rows, "ten", split_axis=1, concat_axis=0, tiled=True)
    row_block = attended
    projected = lax.psum_scatter(
        jnp.dot(row_block, out_proj, preferred_element_type=jnp.float32).astype(jnp.bfloat16),
        "ten",
        scatter_dimension=0,
        tiled=True,
    ).astype(jnp.float32)
    residual = hidden_in.astype(jnp.float32) + projected
    mean_square = jnp.mean(residual * residual, axis=1, keepdims=True)
    normed = (residual * lax.rsqrt(mean_square + 1e-05) * norm_gain).astype(jnp.bfloat16)
    logits = jnp.dot(normed, router_w, preferred_element_type=jnp.float32)
    experts = router_w.shape[1]
    chosen_hot = (expert_ids[:, :, None] == jnp.arange(experts, dtype=jnp.int32)).astype(jnp.int32)
    chosen_logits = jnp.sum(jnp.where(chosen_hot == 1, logits[:, None, :], 0.0), axis=2)
    route_weights = jax.nn.softmax(chosen_logits, axis=1)
    flat_hot = chosen_hot.reshape(rows_dev * 2, experts)
    slot_rank = jnp.sum((jnp.cumsum(flat_hot, axis=0) - flat_hot) * flat_hot, axis=1).reshape(
        rows_dev, 2
    )
    capacity = CAP
    slot_index = jnp.arange(capacity, dtype=jnp.int32)
    assignment = chosen_hot[:, :, :, None] * (slot_rank[:, :, None, None] == slot_index).astype(
        jnp.int32
    )
    placement = jnp.sum(assignment, axis=1)
    local_experts = experts // groups
    placement_split = placement.reshape(rows_dev, groups, local_experts, capacity).astype(
        jnp.bfloat16
    )
    outgoing = jnp.einsum(
        "rnlc,rd->lncd", placement_split, normed, preferred_element_type=jnp.float32
    ).astype(jnp.bfloat16)
    arrived = lax.all_to_all(outgoing, "exp", split_axis=1, concat_axis=1, tiled=True)
    shard_rows = lax.all_gather(arrived, "ten", axis=1, tiled=True)
    gate_act = jnp.einsum("lscd,ldf->lscf", shard_rows, w_gate, preferred_element_type=jnp.float32)
    up_act = jnp.einsum("lscd,ldf->lscf", shard_rows, w_up, preferred_element_type=jnp.float32)
    hidden = (jax.nn.silu(gate_act) * up_act).astype(jnp.bfloat16)
    row_block = hidden
    summed = lax.psum_scatter(
        jnp.einsum("lscf,lfd->slcd", row_block, w_down, preferred_element_type=jnp.float32).astype(
            jnp.bfloat16
        ),
        "ten",
        scatter_dimension=0,
        tiled=True,
    )
    returned = lax.all_to_all(summed, "exp", split_axis=0, concat_axis=0, tiled=True)
    outputs = returned.reshape(experts * capacity, model_width).astype(jnp.float32)
    weight_map = jnp.sum(
        assignment.astype(jnp.float32) * route_weights[:, :, None, None], axis=1
    ).reshape(rows_dev, experts * capacity)
    expert_mix = jnp.dot(
        weight_map, outputs, precision=lax.Precision.HIGHEST, preferred_element_type=jnp.float32
    )
    return (residual + expert_mix).astype(jnp.bfloat16)


def solution(mesh):
    in_specs = (
        P(("rep", "exp", "ten"), None),
        P(("rep", "exp", "ten"), None),
        P(None, ("rep", "exp", "ten"), None),
        P(None, ("rep", "exp"), "ten", None),
        P(None, ("rep", "exp", "ten"), None, None),
        P(("rep", "exp")),
        P(("rep", "exp", "ten")),
        P("ten", None),
        P(),
        P(),
        P(("rep", "exp", "ten"), None),
        P("exp", None, "ten"),
        P("exp", None, "ten"),
        P("exp", "ten", None),
    )
    out_specs = P(("rep", "exp", "ten"), None)
    return jax.shard_map(
        on_device, mesh=mesh, in_specs=in_specs, out_specs=out_specs, check_vma=False
    )
```

profile of v0, /device:TPU:0, one launch (start us, length us, event | category | flops | bytes accessed | tf_op | source)
XLA Modules:
  0.0 201.0 jit_solution(10028590843201728159)
XLA Ops:
  6.6 0.8 fusion.119
  7.3 1.2 fusion.117
  8.6 0.1 copy.127
  8.7 0.1 copy.98
  8.8 0.1 slice.49
  8.9 0.1 copy.126
  8.9 0.1 copy.96
  9.0 0.3 copy-done.14
  9.3 0.1 fusion.79
  9.4 0.5 fusion.120
  9.9 0.1 copy.100
  10.0 0.1 copy.122
  10.1 7.6 %all_gather.10 = bf16[2,80,1024]{2,0,1:T(2,128)(2,1)S(1)} all-gather(bf16[2,20,1024]{2,0,1:T(2,128)(2,1)S(1)} %copy.122), channel_id=1, replica_groups=mesh['rep'=2,'exp'=4,'ten'=4] {'ten'}, dimensions={1}, use_global_device_ids=true | all-gather | bytes 409600 | tf_op jit(solution)/shard_map/all_gather | solution.py:71
  17.7 1.4 slice_reduce_fusion
  19.1 0.1 copy.87
  19.3 7.3 %all-gather = bf16[2,1,128,1024]{3,0,1,2:T(2,128)(2,1)S(1)} all-gather(bf16[2,1,32,1024]{3,0,1,2:T(2,128)(2,1)S(1)} %copy.87), channel_id=2, replica_groups=mesh['rep'=2,'exp'=4,'ten'=4] {'ten'}, dimensions={2}, use_global_device_ids=true | all-gather | bytes 655360 | tf_op jit(solution)/shard_map/all_gather | solution.py:70
  26.6 0.7 fusion.118
  27.3 0.4 copy.121
  27.8 0.2 copy.90
  28.6 0.4 copy.123
  29.1 0.2 copy.93
  29.3 0.3 slice.45
  29.6 0.5 fusion.49
  30.1 0.1 fusion.61
  30.3 0.1 copy_bitcast_fusion
  30.3 0.1 compare_select_fusion
  30.4 0.7 fusion.123
  31.2 0.8 fusion.35
  31.9 0.1 pad_maximum_fusion
  32.0 0.1 copy.102
  32.1 0.2 convert_element_type.72
  32.3 0.1 copy.103
  32.3 8.8 %all_to_all.26 = bf16[24,4,1536]{2,0,1:T(8,128)(2,1)S(1)} all-to-all(bf16[24,4,1536]{2,0,1:T(8,128)(2,1)S(1)} %copy.103), channel_id=1, replica_groups=mesh['rep'=2,'exp'=4,'ten'=4] {'ten'}, dimensions={1} | all-to-all | bytes 589824 | tf_op jit(solution)/shard_map/all_to_all | solution.py:107
  41.1 6.2 %convolution_convert_fusion = bf16[96,3072]{1,0:T(8,128)(2,1)} fusion(bf16[96,1536]{1,0:T(8,128)(2,1)S(1)} %bitcast.127, bf16[1536,3072]{1,0:T(8,128)(2,1)} %param.21), kind=kOutput, calls=%fused_computation.10 | convolution fusion | flops 906264576 | bytes 10321920 | tf_op jit(solution)/shard_map/dot_general | solution.py:110
  47.5 0.1 copy.104
  47.5 0.1 eq.68
  47.6 0.1 fusion.69
  47.7 0.1 reduce_window_sum.11
  47.8 0.2 select_reduce_fusion
  48.0 0.1 eq.72
  48.1 0.1 copy.105
  48.2 0.6 copy-done.7
  48.8 0.6 copy-done.9
  49.4 20.6 %reduce-scatter.3.cloned.1.call-done = bf16[24,3072]{1,0:T(8,128)(2,1)} async-done(((bf16[96,3072]{1,0:T(8,128)(2,1)}), bf16[24,3072]{1,0:T(8,128)(2,1)}) %reduce-scatter.3.cloned.1.call-update) | async-done | bytes 147472 | tf_op jit(solution)/shard_map/reduce_scatter | solution.py:109
  70.0 1.1 multiply_reduce_fusion
  71.0 1.0 multiply_convert_fusion
  72.1 0.2 fusion.14
  72.3 0.4 copy.108
  72.7 14.9 %all_to_all.27 = bf16[2,4,7,3072]{3,0,2,1:T(2,128)(2,1)} all-to-all(bf16[2,4,7,3072]{3,0,2,1:T(2,128)(2,1)S(1)} %copy.108), channel_id=1, replica_groups=mesh['rep'=2,'exp'=4,'ten'=4] {'exp'}, dimensions={1} | all-to-all | bytes 688128 | tf_op jit(solution)/shard_map/all_to_all | solution.py:140
  87.7 0.2 all-reduce.3.cloned.1.call-start
  87.9 16.6 %all-gather.3.cloned.1.call-done = bf16[2,16,7,3072]{3,0,2,1:T(2,128)(2,1)} async-done(((bf16[2,4,7,3072]{3,0,2,1:T(2,128)(2,1)}), bf16[2,16,7,3072]{3,0,2,1:T(2,128)(2,1)}) %all-gather.3.cloned.1.call-update) | async-done | bytes 1376272 | tf_op jit(solution)/shard_map/all_gather | solution.py:141
  104.5 10.9 %fusion.6 = f32[2,16,7,2048]{3,1,2,0:T(8,128)S(1)} fusion(bf16[2,3072,2048]{2,1,0:T(8,128)(2,1)} %param.25, bf16[2,16,7,3072]{3,0,2,1:T(2,128)(2,1)} %all-gather.3.cloned.1.call-done), kind=kOutput, calls=%fused_computation.6 | convolution fusion | flops 2818572288 | bytes 28377088 | tf_op jit(solution)/shard_map/lscd,ldf->lscf/dot_general | solution.py:142
  115.4 20.2 %fusion.11 = bf16[16,2,7,3072]{3,0,2,1:T(8,128)(2,1)} fusion(bf16[2,2048,3072]{2,1,0:T(8,128)(2,1)} %param.27, bf16[2,3072,2048]{2,1,0:T(8,128)(2,1)} %param.26, f32[2,16,7,2048]{3,1,2,0:T(8,128)S(1)} %fusion.6, bf16[2,16,7,3072]{3,0,2,1:T(2,128)(2,1)S(1)} %copy-done.1), kind=kOutput, calls=%fused_computation.9 | convolution fusion | flops 5640585216 | bytes 54919168 | tf_op jit(solution)/shard_map/lscf,lfd->slcd/dot_general | solution.py:147
  135.7 0.6 copy-done.15
  136.3 0.6 dynamic-slice
  137.6 0.2 fusion.126
  137.7 38.1 %all-reduce.3.cloned.1.call-done = bf16[16,2,7,3072]{3,0,2,1:T(8,128)(2,1)} async-done(((bf16[16,2,7,3072]{3,0,2,1:T(8,128)(2,1)}), bf16[16,2,7,3072]{3,0,2,1:T(8,128)(2,1)}) %all-reduce.3.cloned.1.call-update) | async-done | bytes 1376272
  175.9 1.3 constant_dynamic-slice_fusion
  177.1 1.0 copy.111
  178.1 4.6 %all-to-all-start.2 = ((bf16[4,2,7,3072]{3,1,2,0:T(2,128)(2,1)}), bf16[4,2,7,3072]{3,1,2,0:T(2,128)(2,1)S(1)}, u32[]{:S(2)}, u32[]{:S(2)}) async-start(bf16[4,2,7,3072]{3,1,2,0:T(2,128)(2,1)} %copy.111), calls=%async_computation.3 | async-start | bytes 688128 | tf_op jit(solution)/shard_map/all_to_all | solution.py:154
  182.9 10.4 %all-to-all-done.2 = bf16[4,2,7,3072]{3,1,2,0:T(2,128)(2,1)S(1)} async-done(((bf16[4,2,7,3072]{3,1,2,0:T(2,128)(2,1)}), bf16[4,2,7,3072]{3,1,2,0:T(2,128)(2,1)S(1)}, u32[]{:S(2)}, u32[]{:S(2)}) %all-to-all-start.2) | async-done | bytes 344096 | tf_op jit(solution)/shard_map/all_to_all | solution.py:154
  193.2 0.1 copy.112
  193.3 0.1 reshape.204
  193.5 1.0 fusion.15
  (52 shorter events, 0.4 us)
Async XLA Ops:
  6.5 131.0 %copy-start = (bf16[3072,8]{0,1:T(8,128)(2,1)S(1)}, bf16[3072,8]{0,1:T(8,128)(2,1)}, u32[]{:S(2)}) copy-start(bf16[3072,8]{0,1:T(8,128)(2,1)} %param.23) | copy-start | bytes 147460
  6.5 63.4 %reduce-scatter.3.cloned.1.call-start = ((), (), s32[]{:S(2)}) async-start(), calls=%async_computation.4 | async-start | bytes 737280 | tf_op jit(solution)/shard_map/reduce_scatter | solution.py:109
  7.3 1.4 copy-start.4
  8.6 0.7 copy-start.14
  8.9 1.2 copy-start.5
  9.4 9.8 %copy-start.6 = (bf16[2,1,32,1024]{3,2,1,0:T(8,128)(2,1)S(1)}, bf16[2,1,32,1024]{3,2,1,0:T(8,128)(2,1)}, u32[]{:S(2)}) copy-start(bf16[2,1,32,1024]{3,2,1,0:T(8,128)(2,1)} %param.17) | copy-start | bytes 393220
  41.1 6.3 %copy-start.12 = (s32[24,2]{0,1:T(2,128)S(1)}, s32[24,2]{0,1:T(2,128)}, u32[]{:S(2)}) copy-start(s32[24,2]{0,1:T(2,128)} %param.24) | copy-start | bytes 580
  41.1 28.8 %copy-start.2 = (bf16[24,3072]{1,0:T(8,128)(2,1)S(1)}, bf16[24,3072]{1,0:T(8,128)(2,1)}, u32[]{:S(2)}) copy-start(bf16[24,3072]{1,0:T(8,128)(2,1)} %param.14) | copy-start | bytes 442372
  41.1 29.9 %copy-start.11 = (f32[3072]{0:T(1024)S(1)}, f32[3072]{0:T(1024)}, u32[]{:S(2)}) copy-start(f32[3072]{0:T(1024)} %param.22) | copy-start | bytes 36868
  47.4 57.1 %all-gather.3.cloned.1.call-start = ((), (), s32[]{:S(2)}) async-start(), calls=%async_computation.5 | async-start | bytes 1720320 | tf_op jit(solution)/shard_map/all_gather | solution.py:141
  48.2 0.6 copy-start.7
  48.8 0.6 copy-start.9
  87.7 88.2 %all-reduce.3.cloned.1.call-start = ((), (), s32[]{:S(2)}) async-start(), calls=%async_computation.6 | async-start | bytes 2752512
  104.5 10.9 %copy-start.1 = (bf16[2,16,7,3072]{3,0,2,1:T(2,128)(2,1)S(1)}, bf16[2,16,7,3072]{3,0,2,1:T(2,128)(2,1)}, u32[]{:S(2)}) copy-start(bf16[2,16,7,3072]{3,0,2,1:T(2,128)(2,1)} %all-gather.3.cloned.1.call-done) | copy-start | bytes 4128772
  135.6 0.7 copy-start.15
  135.7 47.1 %copy-start.13 = (s32[24,2]{0,1:T(2,128)S(1)}, s32[24,2]{0,1:T(2,128)}, u32[]{:S(2)}) copy-start(s32[24,2]{0,1:T(2,128)} %param.24) | copy-start | bytes 580
  135.7 47.1 %copy-start.8 = (s32[24,2,8]{0,2,1:T(8,128)S(1)}, s32[24,2,8]{0,2,1:T(8,128)}, u32[]{:S(2)}) copy-start(s32[24,2,8]{0,2,1:T(8,128)} %copy-done.7) | copy-start | bytes 4612
  135.7 47.1 %copy-start.10 = (s32[24,2,7]{0,2,1:T(8,128)S(1)}, s32[24,2,7]{0,2,1:T(8,128)}, u32[]{:S(2)}) copy-start(s32[24,2,7]{0,2,1:T(8,128)} %copy-done.9) | copy-start | bytes 4036
  177.1 16.3 %copy-start.3 = (bf16[24,3072]{1,0:T(8,128)(2,1)S(1)}, bf16[24,3072]{1,0:T(8,128)(2,1)}, u32[]{:S(2)}) copy-start(bf16[24,3072]{1,0:T(8,128)(2,1)} %reduce-scatter.3.cloned.1.call-done) | copy-start | bytes 442372
  178.1 15.1 %all-to-all-start.2 = ((bf16[4,2,7,3072]{3,1,2,0:T(2,128)(2,1)}), bf16[4,2,7,3072]{3,1,2,0:T(2,128)(2,1)S(1)}, u32[]{:S(2)}, u32[]{:S(2)}) async-start(bf16[4,2,7,3072]{3,1,2,0:T(2,128)(2,1)} %copy.111), calls=%async_computation.3 | async-start | bytes 688128 | tf_op jit(solution)/shard_map/all_to_all | solution.py:154
Sparse Core Ops, SparseCore 0:
  47.5 22.3 reduce-scatter.2
  87.8 16.6 all-gather.2
  135.8 40.0 all-reduce.2
where the time goes:
time: 201 us
  waiting for transfers between devices  85.7 us (43%)
  matrix products  41.3 us (21%)
  blocking collectives  38.6 us (19%)
  between operations  14.8 us (7%)
  local copies, waits for them, and re-layouts  12.7 us (6%)
  starting transfers between devices  4.87 us (2%)
  other arithmetic  2.9 us (1%)
    unnamed x4, waiting for transfers between devices  38.2 us
    reduce_scatter x1, waiting for transfers between devices, on_device(): lax.psum_scatter(jnp.dot(row_block, out_proj, preferred_element_type=jnp....  20.6 us
    dot_general x1, matrix products, on_device(): jnp.einsum('lscf,lfd->slcd', row_block, w_down, preferred_element_type=jn...  20.2 us
    all_gather x1, waiting for transfers between devices, on_device(): shard_rows = lax.all_gather(arrived, 'ten', axis=1, tiled=True)  16.6 us
    all_to_all x1, blocking collectives, on_device(): lax.all_to_all(outgoing, 'exp', split_axis=1, concat_axis=1, tiled=True)  14.9 us
    dot_general x1, matrix products, on_device(): jnp.einsum('lscd,ldf->lscf', shard_rows, w_gate, preferred_element_type=j...  10.9 us
    all_to_all x1, waiting for transfers between devices, on_device(): lax.all_to_all(summed, 'exp', split_axis=0, concat_axis=0, tiled=True)  10.4 us
    all_to_all x1, blocking collectives, on_device(): lax.all_to_all(attended_rows, 'ten', split_axis=1, concat_axis=0, tiled=T...  8.78 us
  transfers between devices with their start and end apart: 4, of which 4 were waited for; matrix products, arithmetic and copies ran while one was open for 1% of the time, Pallas kernels for 0%

commit v1 on v0

--- a/solution.py
+++ b/solution.py
@@ -151,7 +151,18 @@
         scatter_dimension=0,
         tiled=True,
     )
-    returned = lax.all_to_all(summed, "exp", split_axis=0, concat_axis=0, tiled=True)
+    ways, here = (lax.axis_size("exp"), lax.axis_index("exp"))
+    width = summed.shape[0] // ways
+    lengths = list(summed.shape)
+    lengths[0] = width
+    height = lengths[0]
+    lengths[0] = height * ways
+    returned = jnp.zeros(lengths, summed.dtype)
+    for mask in range(ways):
+        part = lax.dynamic_slice_in_dim(summed, (here ^ mask) * width, width, axis=0)
+        if mask:
+            part = lax.ppermute(part, "exp", [(d, d ^ mask) for d in range(ways)])
+        returned = lax.dynamic_update_slice_in_dim(returned, part, (here ^ mask) * height, axis=0)
     outputs = returned.reshape(experts * capacity, model_width).astype(jnp.float32)
     weight_map = jnp.sum(
         assignment.astype(jnp.float32) * route_weights[:, :, None, None], axis=1

time: 201 us -> 204 us (1.015)
    ppermute x0 -> x3, waiting for transfers between devices: none -> 12.5 us  [on_device(): part = lax.ppermute(part, 'exp', [(d, d ^ mask) for d in range(ways)])]
    all_to_all x1 -> x0, waiting for transfers between devices: 10.4 us -> none  [on_device(): lax.all_to_all(summed, 'exp', split_axis=0, concat_axis=0, tiled=True)]
    all_to_all x1 -> x0, starting transfers between devices: 4.6 us -> none  [on_device(): lax.all_to_all(summed, 'exp', split_axis=0, concat_axis=0, tiled=True)]
    ppermute x0 -> x3, starting transfers between devices: none -> 4.45 us  [on_device(): part = lax.ppermute(part, 'exp', [(d, d ^ mask) for d in range(ways)])]
    dynamic_slice x0 -> x1, local copies, waits for them, and re-layouts: none -> 2.65 us  [on_device(): lax.dynamic_slice_in_dim(summed, (here ^ mask) * width, width, axis=0)]
    unnamed x41 -> x40, local copies, waits for them, and re-layouts: 5.37 us -> 4.93 us
  transfers between devices with their start and end apart: 4 -> 6, of which waited for: 4 -> 5; matrix products, arithmetic and copies ran while one was open for 1% -> 1% of each run, Pallas kernels for 0% -> 0%
where the time goes in v1:
time: 204 us; the launch traced here: 203 us
  waiting for transfers between devices  87.7 us (43%)
  matrix products  41.3 us (20%)
  blocking collectives  38.6 us (19%)
  between operations  14.9 us (7%)
  local copies, waits for them, and re-layouts  13 us (6%)
  starting transfers between devices  4.72 us (2%)
  other arithmetic  2.91 us (1%)
    unnamed x4, waiting for transfers between devices  39.4 us
    reduce_scatter x1, waiting for transfers between devices, on_device(): lax.psum_scatter(jnp.dot(row_block, out_proj, preferred_element_type=jnp....  20.6 us
    dot_general x1, matrix products, on_device(): jnp.einsum('lscf,lfd->slcd', row_block, w_down, preferred_element_type=jn...  20.2 us
    all_gather x1, waiting for transfers between devices, on_device(): shard_rows = lax.all_gather(arrived, 'ten', axis=1, tiled=True)  15.2 us
    all_to_all x1, blocking collectives, on_device(): lax.all_to_all(outgoing, 'exp', split_axis=1, concat_axis=1, tiled=True)  15 us
    ppermute x3, waiting for transfers between devices, on_device(): part = lax.ppermute(part, 'exp', [(d, d ^ mask) for d in range(ways)])  12.5 us
    dot_general x1, matrix products, on_device(): jnp.einsum('lscd,ldf->lscf', shard_rows, w_gate, preferred_element_type=j...  10.9 us
    all_to_all x1, blocking collectives, on_device(): lax.all_to_all(attended_rows, 'ten', split_axis=1, concat_axis=0, tiled=T...  8.77 us
  transfers between devices with their start and end apart: 6, of which 5 were waited for; matrix products, arithmetic and copies ran while one was open for 1% of the time, Pallas kernels for 0%

profile of v1, /device:TPU:0, one launch (start us, length us, event | category | flops | bytes accessed | tf_op | source)
XLA Modules:
  0.0 203.2 jit_solution(1401745576272824365)
XLA Ops:
  6.6 0.8 fusion.119
  7.4 1.0 copy.105
  8.3 7.6 %all_gather.10 = bf16[2,80,1024]{2,0,1:T(2,128)(2,1)S(1)} all-gather(bf16[2,20,1024]{2,0,1:T(2,128)(2,1)S(1)} %copy.105), channel_id=1, replica_groups=mesh['rep'=2,'exp'=4,'ten'=4] {'ten'}, dimensions={1}, use_global_device_ids=true | all-gather | bytes 409600 | tf_op jit(solution)/shard_map/all_gather | solution.py:71
  15.9 1.4 slice_reduce_fusion
  18.0 0.1 copy.68
  18.2 7.3 %all-gather = bf16[2,1,128,1024]{3,0,1,2:T(2,128)(2,1)S(1)} all-gather(bf16[2,1,32,1024]{3,0,1,2:T(2,128)(2,1)S(1)} %copy.68), channel_id=2, replica_groups=mesh['rep'=2,'exp'=4,'ten'=4] {'ten'}, dimensions={2}, use_global_device_ids=true | all-gather | bytes 655360 | tf_op jit(solution)/shard_map/all_gather | solution.py:70
  25.5 0.7 fusion.118
  26.2 0.4 copy.106
  26.7 0.2 copy.74
  26.9 0.3 slice.45
  27.2 0.4 copy.104
  27.7 0.2 copy.71
  27.9 0.1 fusion.117
  28.0 0.1 copy.109
  28.0 0.1 copy.77
  28.1 0.1 copy.110
  28.2 0.1 copy.79
  28.3 0.1 slice.49
  28.3 0.3 copy-done.14
  28.7 0.1 fusion.79
  28.8 0.5 fusion.120
  29.3 0.1 copy.81
  29.4 0.1 copy_bitcast_fusion
  29.5 0.5 fusion.49
  30.0 0.1 fusion.61
  30.2 0.1 compare_select_fusion
  30.2 0.7 fusion.123
  31.0 0.8 fusion.35
  31.7 0.1 pad_maximum_fusion
  31.8 0.1 copy.83
  31.9 0.2 convert_element_type.72
  32.2 8.8 %all_to_all.21 = bf16[24,4,1536]{2,0,1:T(8,128)(2,1)S(1)} all-to-all(bf16[24,4,1536]{2,0,1:T(8,128)(2,1)S(1)} %copy.84), channel_id=1, replica_groups=mesh['rep'=2,'exp'=4,'ten'=4] {'ten'}, dimensions={1} | all-to-all | bytes 589824 | tf_op jit(solution)/shard_map/all_to_all | solution.py:107
  40.9 6.3 %convolution_convert_fusion = bf16[96,3072]{1,0:T(8,128)(2,1)} fusion(bf16[96,1536]{1,0:T(8,128)(2,1)S(1)} %bitcast.127, bf16[1536,3072]{1,0:T(8,128)(2,1)} %param.21), kind=kOutput, calls=%fused_computation.10 | convolution fusion | flops 906264576 | bytes 10321920 | tf_op jit(solution)/shard_map/dot_general | solution.py:110
  47.3 0.1 copy.85
  47.4 0.1 eq.68
  47.5 0.1 fusion.69
  47.5 0.1 reduce_window_sum.11
  47.6 0.2 select_reduce_fusion
  47.8 0.1 eq.72
  47.9 0.1 copy.86
  48.0 0.6 copy-done.7
  48.6 0.6 copy-done.9
  49.2 20.6 %reduce-scatter.3.cloned.1.call-done = bf16[24,3072]{1,0:T(8,128)(2,1)} async-done(((bf16[96,3072]{1,0:T(8,128)(2,1)}), bf16[24,3072]{1,0:T(8,128)(2,1)}) %reduce-scatter.3.cloned.1.call-update) | async-done | bytes 147472 | tf_op jit(solution)/shard_map/reduce_scatter | solution.py:109
  69.8 1.1 multiply_reduce_fusion
  70.9 1.0 multiply_convert_fusion
  71.9 0.2 fusion.14
  72.1 0.4 copy.89
  72.5 15.0 %all_to_all.22 = bf16[2,4,7,3072]{3,0,2,1:T(2,128)(2,1)} all-to-all(bf16[2,4,7,3072]{3,0,2,1:T(2,128)(2,1)S(1)} %copy.89), channel_id=1, replica_groups=mesh['rep'=2,'exp'=4,'ten'=4] {'exp'}, dimensions={1} | all-to-all | bytes 688128 | tf_op jit(solution)/shard_map/all_to_all | solution.py:140
  87.5 0.2 all-reduce.3.cloned.1.call-start
  87.8 0.7 dynamic-slice
  89.1 15.2 %all-gather.3.cloned.1.call-done = bf16[2,16,7,3072]{3,0,2,1:T(2,128)(2,1)} async-done(((bf16[2,4,7,3072]{3,0,2,1:T(2,128)(2,1)}), bf16[2,16,7,3072]{3,0,2,1:T(2,128)(2,1)}) %all-gather.3.cloned.1.call-update) | async-done | bytes 1376272 | tf_op jit(solution)/shard_map/all_gather | solution.py:141
  104.3 10.9 %fusion.6 = f32[2,16,7,2048]{3,1,2,0:T(8,128)S(1)} fusion(bf16[2,3072,2048]{2,1,0:T(8,128)(2,1)} %param.25, bf16[2,16,7,3072]{3,0,2,1:T(2,128)(2,1)} %all-gather.3.cloned.1.call-done), kind=kOutput, calls=%fused_computation.6 | convolution fusion | flops 2818572288 | bytes 28377088 | tf_op jit(solution)/shard_map/lscd,ldf->lscf/dot_general | solution.py:142
  115.3 20.2 %fusion.11 = bf16[16,2,7,3072]{3,0,2,1:T(8,128)(2,1)} fusion(bf16[2,2048,3072]{2,1,0:T(8,128)(2,1)} %param.27, bf16[2,3072,2048]{2,1,0:T(8,128)(2,1)} %param.26, f32[2,16,7,2048]{3,1,2,0:T(8,128)S(1)} %fusion.6, bf16[2,16,7,3072]{3,0,2,1:T(2,128)(2,1)S(1)} %copy-done.1), kind=kOutput, calls=%fused_computation.9 | convolution fusion | flops 5640585216 | bytes 54919168 | tf_op jit(solution)/shard_map/lscf,lfd->slcd/dot_general | solution.py:147
  135.5 0.2 fusion.126
  135.7 0.5 copy-done.13
  136.3 39.4 %all-reduce.3.cloned.1.call-done = bf16[16,2,7,3072]{3,0,2,1:T(8,128)(2,1)} async-done(((bf16[16,2,7,3072]{3,0,2,1:T(8,128)(2,1)}), bf16[16,2,7,3072]{3,0,2,1:T(8,128)(2,1)}) %all-reduce.3.cloned.1.call-update) | async-done | bytes 1376272
  175.7 2.6 %constant_dynamic-slice_fusion.3 = (bf16[1,2,7,3072]{3,0,2,1:T(2,128)(2,1)S(1)}, bf16[1,2,7,3072]{3,0,2,1:T(2,128)(2,1)S(1)}, bf16[1,2,7,3072]{3,0,2,1:T(2,128)(2,1)S(1)}, bf16[1,2,7,3072]{3,0,2,1:T(2,128)(2,1)S(1)}) fusion(bf16[16,2,7,3072]{3,0,2,1:T(8,128)(2,1)} %all-reduce.3.cloned.1.call-done, s32[]{:T(128)S(6)} %add.79, s32[]{:T(128)S(6)} %add.75, ...), kind=kLoop, calls=%fused_computation.88 | loop fusion | bytes 688144 | tf_op jit(solution)/shard_map/dynamic_slice | solution.py:162
  178.4 1.6 collective-permute-start
  179.9 2.4 %collective-permute-start.1 = (bf16[1,2,7,3072]{3,0,2,1:T(2,128)(2,1)S(1)}, bf16[1,2,7,3072]{3,0,2,1:T(2,128)(2,1)S(1)}, u32[]{:S(2)}, u32[]{:S(2)}) collective-permute-start(bf16[1,2,7,3072]{3,0,2,1:T(2,128)(2,1)S(1)} %get-tuple-element.8), channel_id=1, source_target_pairs={{0,8},{4,12},{8,0},{12,4},{1,9},{5,13},{9,1},{13,5},{2,10},{6,14},... | collective-permute-start | bytes 258056 | tf_op jit(solution)/shard_map/ppermute | solution.py:164
  182.3 0.5 collective-permute-start.2
  182.9 4.2 %collective-permute-done = bf16[1,2,7,3072]{3,0,2,1:T(2,128)(2,1)S(1)} collective-permute-done((bf16[1,2,7,3072]{3,0,2,1:T(2,128)(2,1)S(1)}, bf16[1,2,7,3072]{3,0,2,1:T(2,128)(2,1)S(1)}, u32[]{:S(2)}, u32[]{:S(2)}) %collective-permute-start) | collective-permute-done | bytes 86048 | tf_op jit(solution)/shard_map/ppermute | solution.py:164
  187.1 8.3 %collective-permute-done.1 = bf16[1,2,7,3072]{3,0,2,1:T(2,128)(2,1)S(1)} collective-permute-done((bf16[1,2,7,3072]{3,0,2,1:T(2,128)(2,1)S(1)}, bf16[1,2,7,3072]{3,0,2,1:T(2,128)(2,1)S(1)}, u32[]{:S(2)}, u32[]{:S(2)}) %collective-permute-start.1) | collective-permute-done | bytes 86048 | tf_op jit(solution)/shard_map/ppermute | solution.py:164
  195.5 0.1 reshape.204
  195.7 1.0 fusion.15
  (59 shorter events, 0.6 us)
Async XLA Ops:
  6.5 129.0 %copy-start = (bf16[3072,8]{0,1:T(8,128)(2,1)S(1)}, bf16[3072,8]{0,1:T(8,128)(2,1)}, u32[]{:S(2)}) copy-start(bf16[3072,8]{0,1:T(8,128)(2,1)} %param.23) | copy-start | bytes 147460
  6.5 11.5 %copy-start.6 = (bf16[2,1,32,1024]{3,2,1,0:T(8,128)(2,1)S(1)}, bf16[2,1,32,1024]{3,2,1,0:T(8,128)(2,1)}, u32[]{:S(2)}) copy-start(bf16[2,1,32,1024]{3,2,1,0:T(8,128)(2,1)} %param.17) | copy-start | bytes 393220
  6.5 63.2 %reduce-scatter.3.cloned.1.call-start = ((), (), s32[]{:S(2)}) async-start(), calls=%async_computation.3 | async-start | bytes 737280 | tf_op jit(solution)/shard_map/reduce_scatter | solution.py:109
  25.5 1.4 copy-start.5
  26.6 1.2 copy-start.4
  28.0 0.7 copy-start.14
  40.9 6.3 %copy-start.12 = (s32[24,2]{0,1:T(2,128)S(1)}, s32[24,2]{0,1:T(2,128)}, u32[]{:S(2)}) copy-start(s32[24,2]{0,1:T(2,128)} %param.24) | copy-start | bytes 580
  40.9 28.8 %copy-start.2 = (bf16[24,3072]{1,0:T(8,128)(2,1)S(1)}, bf16[24,3072]{1,0:T(8,128)(2,1)}, u32[]{:S(2)}) copy-start(bf16[24,3072]{1,0:T(8,128)(2,1)} %param.14) | copy-start | bytes 442372
  40.9 29.9 %copy-start.11 = (f32[3072]{0:T(1024)S(1)}, f32[3072]{0:T(1024)}, u32[]{:S(2)}) copy-start(f32[3072]{0:T(1024)} %param.22) | copy-start | bytes 36868
  47.2 57.1 %all-gather.3.cloned.1.call-start = ((), (), s32[]{:S(2)}) async-start(), calls=%async_computation.4 | async-start | bytes 1720320 | tf_op jit(solution)/shard_map/all_gather | solution.py:141
  48.0 0.6 copy-start.7
  48.6 0.6 copy-start.9
  70.8 16.9 %copy-start.15 = (u32[32]{0:T(128)S(1)}, u32[32]{0:T(128)}, u32[]{:S(2)}) copy-start(u32[32]{0:T(128)} %constant.63) | copy-start | bytes 388
  87.5 88.2 %all-reduce.3.cloned.1.call-start = ((), (), s32[]{:S(2)}) async-start(), calls=%async_computation.5 | async-start | bytes 2752512
  104.3 10.9 %copy-start.1 = (bf16[2,16,7,3072]{3,0,2,1:T(2,128)(2,1)S(1)}, bf16[2,16,7,3072]{3,0,2,1:T(2,128)(2,1)}, u32[]{:S(2)}) copy-start(bf16[2,16,7,3072]{3,0,2,1:T(2,128)(2,1)} %all-gather.3.cloned.1.call-done) | copy-start | bytes 4128772
  135.5 0.7 copy-start.13
  135.5 0.8 copy-start.8
  135.5 0.8 copy-start.10
  178.3 17.3 %copy-start.3 = (bf16[24,3072]{1,0:T(8,128)(2,1)S(1)}, bf16[24,3072]{1,0:T(8,128)(2,1)}, u32[]{:S(2)}) copy-start(bf16[24,3072]{1,0:T(8,128)(2,1)} %reduce-scatter.3.cloned.1.call-done) | copy-start | bytes 442372
  178.4 8.7 %collective-permute-start = (bf16[1,2,7,3072]{3,0,2,1:T(2,128)(2,1)S(1)}, bf16[1,2,7,3072]{3,0,2,1:T(2,128)(2,1)S(1)}, u32[]{:S(2)}, u32[]{:S(2)}) collective-permute-start(bf16[1,2,7,3072]{3,0,2,1:T(2,128)(2,1)S(1)} %get-tuple-element.9), channel_id=1, source_target_pairs={{0,4},{4,0},{8,12},{12,8},{1,5},{5,1},{9,13},{13,9},{2,6},{6,2},{1... | collective-permute-start | bytes 258056 | tf_op jit(solution)/shard_map/ppermute | solution.py:164
  179.9 15.5 %collective-permute-start.1 = (bf16[1,2,7,3072]{3,0,2,1:T(2,128)(2,1)S(1)}, bf16[1,2,7,3072]{3,0,2,1:T(2,128)(2,1)S(1)}, u32[]{:S(2)}, u32[]{:S(2)}) collective-permute-start(bf16[1,2,7,3072]{3,0,2,1:T(2,128)(2,1)S(1)} %get-tuple-element.8), channel_id=1, source_target_pairs={{0,8},{4,12},{8,0},{12,4},{1,9},{5,13},{9,1},{13,5},{2,10},{6,14},... | collective-permute-start | bytes 258056 | tf_op jit(solution)/shard_map/ppermute | solution.py:164
  182.3 13.2 %collective-permute-start.2 = (bf16[1,2,7,3072]{3,0,2,1:T(2,128)(2,1)S(1)}, bf16[1,2,7,3072]{3,0,2,1:T(2,128)(2,1)S(1)}, u32[]{:S(2)}, u32[]{:S(2)}) collective-permute-start(bf16[1,2,7,3072]{3,0,2,1:T(2,128)(2,1)S(1)} %get-tuple-element.7), channel_id=1, source_target_pairs={{0,12},{4,8},{8,4},{12,0},{1,13},{5,9},{9,5},{13,1},{2,14},{6,10},... | collective-permute-start | bytes 258056 | tf_op jit(solution)/shard_map/ppermute | solution.py:164
Sparse Core Ops, SparseCore 0:
  47.3 22.3 reduce-scatter.2
  87.6 16.6 all-gather.2
  135.6 40.0 all-reduce.2
